TPU v7x, 32 devices: a whole 2x2x4 slice. The times are simulated.
32 devices in a mesh: coil: 8 (over y, x, core), kz: 4 (over z).
Axes of the slice: x: 2, y: 2, z: 4, core: 2. Of those that a mesh axis runs over, the one named last changes fastest.
Arguments:
- kdata: bfloat16 [2, 64, 8, 256, 512], P(None, 'kz', 'coil'), may hold values from -6 to 6
- spoke_angle: int32 [256], replicated, may hold values from 0 to 63
- spoke_count: int32 [64], P('kz'), may hold values from 128 to 256
- block_index: int32 [64, 4], replicated, may hold values from 0 to 511
- interp: bfloat16 [64, 4, 128, 128], replicated, may hold values from -0.5 to 0.5
- sens_maps: bfloat16 [2, 8, 256, 256], P(None, 'coil'), may hold values from -5 to 5
Outputs:
- image: float32 [2, 64, 256, 256], P(None, 'kz', 'coil')
Inputs may be any that keep to these rules, and one draw needn't show every extreme that they name: Partition p uses its first spoke_count[p] spokes. `block_index`: several segments may hit the same grid block.
All inputs are finite; a program needn't handle non-finite values.
Results may differ from a plain program's by a relative error of at most 0.0059.
Values sent between devices are 32-bit elements; how exact they have to be, the bound alone decides.
A program may use at most 128 MiB of HBM per device.

v0:
```python
import functools
import math

import jax
import jax.numpy as jnp
from jax import lax
from jax.experimental import pallas as pl
from jax.experimental.pallas import tpu as pltpu
from jax.sharding import PartitionSpec as P

F32 = jnp.float32
BF16 = jnp.bfloat16
SUB = 2
SUBLANE, LANE = 8, 128


def cos_sin(product, length, dtype):
    phase = (product % length).astype(F32) * (2.0 * jnp.pi / length)
    scale = 1.0 / jnp.sqrt(F32(length))
    return ((jnp.cos(phase) * scale).astype(dtype), (jnp.sin(phase) * scale).astype(dtype))


def halving_orders(bits):
    first = list(range(bits))
    return [first, first[:1] + first[:0:-1]]


def kernel(bits, groups, parts, rows, side, *refs):
    contrib, ymat, xmat, sens, twiddle, out = refs[:6]
    weighted, raw, part_out, part_in = refs[6:10]
    inbox = refs[10 : 10 + bits]
    first_send, first_recv, half_send, half_recv, line_send, line_recv = refs[10 + bits :]
    blocks = 1 << bits
    orders = halving_orders(bits)
    lanes = side // LANE
    steps = rows // SUBLANE
    coil = lax.axis_index("coil")
    kz = lax.axis_index("kz")
    my_bit = [(coil // (1 << bit)) % 2 for bit in range(bits)]
    partner = [coil + (1 - 2 * my_bit[bit]) * (1 << bit) for bit in range(bits)]
    last = groups - 1
    inner = (kz > 0) & (kz < last)
    outer = (kz == 0) | (kz == last)
    inward = jnp.where(kz < 2, kz + 1, kz - 1)
    outward = jnp.where(kz < 2, 0, last)
    far_end = last - outward

    barrier = pltpu.get_barrier_semaphore()
    for bit in range(bits):
        pl.semaphore_signal(barrier, 1, device_id={"coil": partner[bit]})
    pl.semaphore_signal(barrier, 1, device_id={"kz": (kz + 1) % groups})
    pl.semaphore_signal(barrier, 1, device_id={"kz": (kz + groups - 1) % groups})
    pl.semaphore_wait(barrier, bits + 2)

    def kept_start(order, stage):
        start = 0
        for s in range(stage):
            start = start + my_bit[order[s]] * (blocks >> (s + 1))
        return start

    half = blocks // 2

    def first_copy(pair):
        span = pl.ds(pair * SUB, SUB)
        return pltpu.make_async_remote_copy(
            src_ref=weighted.at[:, pl.ds((1 - my_bit[0]) * half, half), span],
            dst_ref=inbox[0].at[:, :, span],
            send_sem=first_send.at[pair],
            recv_sem=first_recv.at[pair],
            device_id={"coil": partner[0]},
        )

    def half_copy(chunk, lane, stage):
        order = orders[lane % 2]
        bit = order[stage]
        size = blocks >> (stage + 1)
        start = kept_start(order, stage) + (1 - my_bit[bit]) * size
        return pltpu.make_async_remote_copy(
            src_ref=weighted.at[chunk, pl.ds(start, size)],
            dst_ref=inbox[stage].at[chunk],
            send_sem=half_send.at[stage - 1, chunk],
            recv_sem=half_recv.at[stage - 1, chunk],
            device_id={"coil": partner[bit]},
        )

    def add_inbox(chunk, lane, stage):
        size = blocks >> (stage + 1)
        start = kept_start(orders[lane % 2], stage + 1)
        for b in range(size):
            total = weighted[chunk, start + b] + inbox[stage][chunk, b]
            if stage < bits - 1:
                weighted[chunk, start + b] = total
            else:
                raw[chunk, kz] = total

    def line_copy(kind, chunk, src, dst, to):
        return pltpu.make_async_remote_copy(
            src_ref=src,
            dst_ref=dst,
            send_sem=line_send.at[kind, chunk],
            recv_sem=line_recv.at[kind, chunk],
            device_id={"kz": to},
        )

    def from_outer(chunk, source):
        return line_copy(0, chunk, raw.at[chunk, source], raw.at[chunk, source], inward)

    def from_inner(chunk, source):
        return line_copy(1, chunk, raw.at[chunk, source], raw.at[chunk, source], inward)

    def forward(chunk, source):
        return line_copy(2, chunk, raw.at[chunk, source], raw.at[chunk, source], inward)

    def partial(chunk):
        return line_copy(3, chunk, part_out.at[chunk], part_in.at[chunk], outward)

    def compute(pair):
        first = pair * SUB
        data = jnp.concatenate([contrib[first + s] for s in range(SUB)], axis=1)
        seg = data.shape[1] // SUB
        halves = [
            jnp.dot(ymat[h], data, preferred_element_type=F32).astype(BF16)
            for h in range(side // seg)
        ]
        s_re = sens[0].astype(F32)
        s_im = sens[1].astype(F32)
        for s in range(SUB):
            pieces = [h[r * side : (r + 1) * side, s * seg : (s + 1) * seg] for r in range(2) for h in halves]
            image = jnp.dot(jnp.concatenate(pieces, axis=1), xmat[...], preferred_element_type=F32)
            i_re, i_im = image[:, :side], image[:, side:]
            result = [s_re * i_re + s_im * i_im, s_re * i_im - s_im * i_re]
            for block in range(blocks):
                for lane in range(lanes):
                    place = 0
                    for bit in orders[lane % 2]:
                        place = place * 2 + (block >> bit) % 2
                    for step in range(steps):
                        top = block * rows + step * SUBLANE
                        for r in range(2):
                            weighted[step * lanes + lane, place, first + s, r] = result[r][
                                top : top + SUBLANE, lane * LANE : (lane + 1) * LANE
                            ]

    def transform(chunk, sources, table, store):
        for q in range(groups):
            sums = []
            for k in range(parts):
                re = im = None
                for j in sources:
                    angle = 2.0 * math.pi * (q * j % groups) / groups
                    c, d = round(math.cos(angle), 12), round(math.sin(angle), 12)
                    x_re, x_im = raw[chunk, j, k, 0], raw[chunk, j, k, 1]
                    for coef, a, b in ((c, x_re, x_im), (d, x_im, -x_re)):
                        if coef == 0.0:
                            continue
                        ta = a if coef == 1.0 else a * F32(coef)
                        tb = b if coef == 1.0 else b * F32(coef)
                        re = ta if re is None else re + ta
                        im = tb if im is None else im + tb
                sums.append((re, im))
            for z in range(q, parts, groups):
                a_re = a_im = None
                for k in range(parts):
                    c, d = twiddle[2 * table, k, z], twiddle[2 * table + 1, k, z]
                    re, im = sums[k]
                    t_re, t_im = c * re + d * im, c * im - d * re
                    a_re = t_re if a_re is None else a_re + t_re
                    a_im = t_im if a_im is None else a_im + t_im
                store(z, a_re, a_im)

    def spot(step, lane):
        return pl.ds(pl.multiple_of(step * SUBLANE, SUBLANE), SUBLANE), pl.ds(lane * LANE, LANE)

    def into_out(step, lane):
        y, x = spot(step, lane)

        def store(z, re, im):
            out[0, z, y, x] = re
            out[1, z, y, x] = im

        return store

    def into_partial(chunk):
        def store(z, re, im):
            part_out[chunk, z, 0] = re
            part_out[chunk, z, 1] = im

        return store

    def each_pair(pair, carry):
        compute(pair)
        first_copy(pair).start()
        return carry

    pairs = parts // SUB
    lax.fori_loop(0, pairs, each_pair, 0)

    def first_wait(pair, carry):
        first_copy(pair).wait_recv()
        return carry

    lax.fori_loop(0, pairs, first_wait, 0)

    def reduce_stage(stage, step):
        for lane in range(lanes):
            chunk = step * lanes + lane
            if stage:
                half_copy(chunk, lane, stage).wait_recv()
            add_inbox(chunk, lane, stage)
            if stage < bits - 1:
                half_copy(chunk, lane, stage + 1).start()
            else:

                @pl.when(outer)
                def _():
                    from_outer(chunk, kz).start()

                @pl.when(inner)
                def _():
                    from_inner(chunk, kz).start()

    def relay_stage(step):
        for lane in range(lanes):
            chunk = step * lanes + lane

            @pl.when(inner)
            def _():
                from_outer(chunk, outward).wait_recv()
                forward(chunk, outward).start()

            for end in (0, last):

                @pl.when(kz == end)
                def _(end=end):
                    transform(chunk, [end], 0, into_out(step, lane))

    def combine_stage(step):
        for lane in range(lanes):
            chunk = step * lanes + lane

            @pl.when(inner)
            def _():
                from_inner(chunk, inward).wait_recv()
                forward(chunk, far_end).wait_recv()

            for place, end in ((1, 0), (last - 1, last)):

                @pl.when(kz == place)
                def _(end=end):
                    transform(chunk, [j for j in range(groups) if j != end], 1, into_partial(chunk))
                    partial(chunk).start()

            @pl.when(inner)
            def _():
                transform(chunk, list(range(groups)), 0, into_out(step, lane))

    def finish_stage(step):
        for lane in range(lanes):
            chunk = step * lanes + lane

            @pl.when(outer)
            def _():
                partial(chunk).wait_recv()
                y, x = spot(step, lane)
                for r in range(2):
                    out[r, :, y, x] = out[r, :, y, x] + part_in[chunk, :, r]

    def tick(t, carry):
        def at(lag, body):
            step = t - lag

            @pl.when((step >= 0) & (step < steps))
            def _():
                body(step)

        at(bits, relay_stage)
        for stage in range(bits - 1, -1, -1):
            at(stage, functools.partial(reduce_stage, stage))
        at(bits + 1, combine_stage)
        at(bits + 2, finish_stage)
        return carry

    lax.fori_loop(0, steps + bits + 2, tick, 0)

    def drain_first(pair, carry):
        first_copy(pair).wait_send()
        return carry

    lax.fori_loop(0, pairs, drain_first, 0)

    def drain(step, carry):
        for lane in range(lanes):
            chunk = step * lanes + lane
            for stage in range(1, bits):
                half_copy(chunk, lane, stage).wait_send()

            @pl.when(outer)
            def _():
                from_outer(chunk, kz).wait_send()

            @pl.when(inner)
            def _():
                from_inner(chunk, kz).wait_send()
                forward(chunk, outward).wait_send()
                partial(chunk).wait_send()

        return carry

    lax.fori_loop(0, steps, drain, 0)


def per_device(kdata, spoke_angle, spoke_count, block_index, interp, sens_maps):
    side = sens_maps.shape[2]
    parts = kdata.shape[1]
    spokes = kdata.shape[3]
    angles, segs, seg = interp.shape[:3]
    coils = lax.axis_size("coil")
    groups = lax.axis_size("kz")
    bits = coils.bit_length() - 1
    rows = side // coils
    length = parts * groups
    kz = lax.axis_index("kz")

    position = jnp.arange(spokes, dtype=jnp.int32)
    used = position[None, :] < spoke_count[:, None]
    match = spoke_angle[:, None] == jnp.arange(angles, dtype=jnp.int32)[None, :]
    weights = (used[:, :, None] & match[None, :, :]).astype(BF16)
    binned = jnp.einsum("rpsn,psa->rpan", kdata[:, :, 0], weights, preferred_element_type=F32).astype(BF16)
    pieces = binned.reshape(2, parts, angles, segs, seg)
    contrib = jnp.einsum("rpagj,agjt->pragt", pieces, interp, preferred_element_type=F32).astype(BF16)
    hits = angles * segs
    contrib = contrib.reshape(parts, 2 * hits, seg)

    across = side // seg
    index = jnp.arange(side, dtype=jnp.int32)
    where = block_index.reshape(-1)
    hit_y = where // across
    hit_x = where % across
    cos_y, sin_y = cos_sin(index[:, None] * hit_y[None, :], side, F32)
    here = (jnp.arange(across, dtype=jnp.int32)[:, None, None] == hit_x).astype(F32)
    cos_y, sin_y = cos_y * here, sin_y * here
    ymat = jnp.concatenate(
        [jnp.concatenate([cos_y, sin_y], 2), jnp.concatenate([-sin_y, cos_y], 2)], 1
    ).astype(BF16)
    cos_x, sin_x = cos_sin(index[:, None] * index[None, :], side, F32)
    xmat = jnp.concatenate(
        [jnp.concatenate([cos_x, -sin_x], 1), jnp.concatenate([sin_x, cos_x], 1)], 0
    ).astype(BF16)
    low = jnp.arange(parts, dtype=jnp.int32)
    outward = jnp.where(kz < 2, 0, groups - 1)
    tables = []
    for owner in (kz, outward):
        tables += cos_sin(low[:, None] * (owner * parts + low)[None, :], length, F32)
    twiddle = jnp.stack(tables)

    assert groups == 4 and parts % groups == 0
    chunks = (rows // SUBLANE) * (side // LANE)
    block = (parts, 2, SUBLANE, LANE)
    vmem = pl.BlockSpec(memory_space=pltpu.VMEM)
    scratch = [
        pltpu.VMEM((chunks, coils) + block, F32),
        pltpu.VMEM((chunks, groups) + block, F32),
        pltpu.VMEM((chunks,) + block, F32),
        pltpu.VMEM((chunks,) + block, F32),
    ]
    scratch += [pltpu.VMEM((chunks, coils >> (s + 1)) + block, F32) for s in range(bits)]
    scratch += [pltpu.SemaphoreType.DMA((parts // SUB,))] * 2
    scratch += [pltpu.SemaphoreType.DMA((bits - 1, chunks))] * 2
    scratch += [pltpu.SemaphoreType.DMA((4, chunks))] * 2
    return pl.pallas_call(
        functools.partial(kernel, bits, groups, parts, rows, side),
        out_shape=jax.ShapeDtypeStruct((2, parts, rows, side), F32),
        in_specs=[vmem] * 4 + [pl.BlockSpec(memory_space=pltpu.SMEM)],
        out_specs=vmem,
        scratch_shapes=scratch,
        compiler_params=pltpu.CompilerParams(
            collective_id=0, has_side_effects=True, vmem_limit_bytes=60 * 1024 * 1024
        ),
        name="combine",
    )(contrib, ymat, xmat, sens_maps[:, 0], twiddle)


def solution(mesh):
    placed = (
        P(None, "kz", "coil", None, None),
        P(),
        P("kz"),
        P(),
        P(),
        P(None, "coil", None, None),
    )
    return jax.shard_map(
        per_device,
        mesh=mesh,
        in_specs=placed,
        out_specs=P(None, "kz", "coil", None),
        check_vma=False,
    )
```

profile of v0, /device:TPU:0, one launch (start us, length us, event | category | flops | bytes accessed | tf_op | source)
XLA Modules:
  0.0 106.8 jit_solution(12699333527203740106)
XLA Ops:
  0.0 0.7 iota_compare_fusion
  0.7 0.7 iota_compare_fusion.1
  1.4 4.9 %convert_bitcast_fusion.1 = bf16[2,16,64,512]{3,2,0,1:T(8,128)(2,1)S(1)} fusion(pred[256,64]{0,1:T(8,128)(4,1)S(1)} %iota_compare_fusion, pred[16,256]{1,0:T(8,128)(4,1)S(1)} %iota_compare_fusion.1, bf16[2,16,1,256,512]{4,3,2,1,0:T(8,128)(2,1)} %param.6), kind=kOutput, calls=%fused_computation.6 | convolution fusion | flops 538181632 | bytes 10506240 | tf_op jit(solution)/shard_map/rpsn,psa->rpan/dot_general | solution.py:328
  6.3 2.1 %reshape.394 = bf16[2,16,64,4,128]{4,3,2,0,1:T(4,128)(2,1)} reshape(bf16[2,16,64,512]{3,2,0,1:T(8,128)(2,1)S(1)} %convert_bitcast_fusion.1) | data formatting | bytes 4194304 | tf_op jit(solution)/shard_map/reshape | solution.py:329
  8.4 6.3 %convert_bitcast_fusion = bf16[16,2,64,4,128]{4,0,1,3,2:T(8,128)(2,1)S(1)} fusion(bf16[64,4,128,128]{3,2,1,0:T(8,128)(2,1)} %param.10, bf16[2,16,64,4,128]{4,3,2,0,1:T(4,128)(2,1)} %reshape.394), kind=kOutput, calls=%fused_computation.5 | convolution fusion | flops 269484032 | bytes 12582912 | tf_op jit(solution)/shard_map/rpagj,agjt->pragt/dot_general | solution.py:330
  14.7 0.0 copy-start
  14.7 2.4 %copy.12 = bf16[16,2,64,4,128]{4,3,2,1,0:T(4,128)(2,1)} copy(bf16[16,2,64,4,128]{4,0,1,3,2:T(8,128)(2,1)S(1)} %convert_bitcast_fusion) | data formatting | bytes 4194304 | tf_op jit(solution)/shard_map/convert_element_type | solution.py:330
  17.1 0.0 copy-done
  17.1 0.1 copy.13
  17.2 0.1 reshape.396
  17.3 1.1 sine_multiply_fusion.1
  18.4 0.1 multiply_convert_fusion
  18.5 1.1 maximum_maximum_fusion.refs_1_
  19.6 1.1 %negate_convert_fusion = (bf16[256,256]{1,0:T(8,128)(2,1)S(1)}, bf16[256,256]{1,0:T(8,128)(2,1)S(1)}) fusion(), kind=kLoop, calls=%fused_computation.29 | loop fusion | flops 1245184 | bytes 262144 | tf_op jit(solution)/shard_map/convert.5
  20.7 1.0 fusion.28
  21.7 0.8 maximum_maximum_fusion.1.refs_2_
  22.5 0.1 cosine_multiply_fusion.1
  22.6 0.6 pad_maximum_fusion.refs_4_
  23.2 81.2 %combine.1 = f32[2,16,32,256]{3,2,1,0:T(8,128)} custom-call(bf16[16,512,128]{2,1,0:T(8,128)(2,1)} %bitcast.26, bf16[2,512,512]{2,1,0:T(8,128)(2,1)} %maximum_maximum_fusion.refs_1_, bf16[512,512]{1,0:T(8,128)(2,1)} %maximum_maximum_fusion.1.refs_2_, bf16[2,256,256]{2,1,0:T(8,128)(2,1)} %bitcast.27, f32[4,16,16]{2,1,0:T(8,128)} %pad_maximum_fusion.refs_4_), custom_call_target="tpu_custom_call" | custom-call | tf_op jit(solution)/shard_map/combine/pallas_call | solution.py:370
  104.5 2.3 %copy.25 = f32[2,16,32,256]{3,2,1,0:T(8,128)} copy(f32[2,16,32,256]{3,2,1,0:T(8,128)} %combine.1) | data formatting | bytes 2097152
  (4 shorter events, 0.0 us)
Async XLA Ops:
  14.7 2.4 %copy-start = (s32[64,4]{0,1:T(4,128)S(1)}, s32[64,4]{0,1:T(4,128)}, u32[]{:S(2)}) copy-start(s32[64,4]{0,1:T(4,128)} %param.9) | copy-start | bytes 3076
where the time goes:
time: 107 us
  Pallas kernels  81.2 us (76%)
  matrix products  11.2 us (10%)
  other arithmetic  7.27 us (7%)
  local copies, waits for them, and re-layouts  7.02 us (7%)
    pallas_call x1, Pallas kernels, per_device(): pl.pallas_call(functools.partial(kernel, bits, groups, parts, rows, side)...  81.2 us
    dot_general x1, matrix products, per_device(): jnp.einsum('rpagj,agjt->pragt', pieces, interp, preferred_element_type=F32)  6.31 us
    dot_general x1, matrix products, per_device(): jnp.einsum('rpsn,psa->rpan', kdata[:, :, 0], weights, preferred_element_t...  4.86 us
    convert_element_type x1, local copies, waits for them, and re-layouts, per_device(): jnp.einsum('rpagj,agjt->pragt', pieces, interp, preferred_element_type=F32)  2.43 us
    unnamed x4, local copies, waits for them, and re-layouts  2.41 us
    another operation x3, other arithmetic  2.19 us

commit v1 on v0

v1 whole, which is shorter than its diff:
```python
import functools
import math

import jax
import jax.numpy as jnp
import numpy as np
from jax import lax
from jax.experimental import pallas as pl
from jax.experimental.pallas import tpu as pltpu
from jax.sharding import PartitionSpec as P

F32 = jnp.float32
BF16 = jnp.bfloat16
I32 = jnp.int32
SUB = 2
SUBLANE, LANE = 8, 128
CUTS = 4
LAG = 2


def cos_sin(product, length):
    phase = (product % length).astype(np.float64) * (2.0 * np.pi / length)
    scale = 1.0 / np.sqrt(length)
    return np.cos(phase) * scale, np.sin(phase) * scale


def halving_orders(bits):
    first = list(range(bits))
    return [first, first[:1] + first[:0:-1]]


def plan(steps, batches, per_batch):
    if steps == 4 and batches == 4 and per_batch == 2:
        half = CUTS // 2
        bins = {0: 0, 4: 1, 7: 2, 9: 3}
        cuts = {0: (0, 0, CUTS), 4: (1, 0, CUTS), 7: (2, 0, half), 8: (2, half, CUTS), 10: (3, 0, CUTS)}
        pairs = {1: (0, 1), 2: (1, 2), 5: (2, 3), 6: (3, 4), 8: (4, 5), 9: (5, 6), 11: (6, 8)}
        items = [(0, s) for s in range(4)] + [(1 + k // 2, k % 2) for k in range(6)] + [(1 + k % 3, 2 + k // 3) for k in range(6)]
        return bins, cuts, pairs, items, [k + 3 if k < 4 else k + 4 for k in range(16)]
    items = [(b, s) for b in range(batches) for s in range(steps)]
    bins = {2 * b: b for b in range(batches)}
    cuts = {2 * b: (b, 0, CUTS) for b in range(batches)}
    pairs = {2 * b + 1: (b * per_batch, (b + 1) * per_batch) for b in range(batches)}
    return bins, cuts, pairs, items, [2 * batches + k for k in range(len(items))]


def kernel(dims, *refs):
    bits, groups, parts, rows, side, angles, segs, seg, spokes = dims
    kdata_in, angle_in, count_in, where_in, interp_in, sens_in, dft_in, twiddle_in, out_hbm = refs[:9]
    kdata, angle, count, where, interp, sens, dft, twiddle = refs[9:17]
    ymat, xmat, match, binned, contrib = refs[17:22]
    weighted, raw, part_out, part_in = refs[22:26]
    inbox = refs[26 : 26 + bits]
    out, small_sem, data_sem, interp_sem, out_sem = refs[26 + bits : 31 + bits]
    sent, first_recv, half_recv, line_recv = refs[31 + bits :]
    blocks = 1 << bits
    orders = halving_orders(bits)
    lanes = side // LANE
    steps = rows // SUBLANE
    share = SUBLANE // 2
    batches = parts // share
    per_batch = share // SUB
    hits = angles * segs
    pitch = hits + SUBLANE
    coil = lax.axis_index("coil")
    kz = lax.axis_index("kz")
    my_bit = [(coil // (1 << bit)) % 2 for bit in range(bits)]
    partner = [coil + (1 - 2 * my_bit[bit]) * (1 << bit) for bit in range(bits)]
    last = groups - 1
    inner = (kz > 0) & (kz < last)
    outer = (kz == 0) | (kz == last)
    inward = jnp.where(kz < 2, kz + 1, kz - 1)
    outward = jnp.where(kz < 2, 0, last)

    smalls = [
        pltpu.make_async_copy(src, dst, small_sem.at[i])
        for i, (src, dst) in enumerate(
            ((angle_in, angle), (count_in, count), (where_in, where), (dft_in, dft), (sens_in, sens), (twiddle_in, twiddle))
        )
    ]

    def data_copy(batch):
        span = pl.ds(batch * share, share)
        return pltpu.make_async_copy(kdata_in.at[:, span], kdata.at[:, span], data_sem.at[batch])

    per_cut = angles // CUTS

    def interp_copy(cut):
        span = pl.ds(cut * per_cut, per_cut)
        return pltpu.make_async_copy(interp_in.at[span], interp.at[span], interp_sem.at[cut])

    for copy in smalls[:2]:
        copy.start()
    data_copy(0).start()
    for copy in smalls[2:]:
        copy.start()
    for cut in range(2):
        interp_copy(cut).start()

    barrier = pltpu.get_barrier_semaphore()
    for bit in range(bits):
        pl.semaphore_signal(barrier, 1, device_id={"coil": partner[bit]})
    pl.semaphore_signal(barrier, 1, device_id={"kz": (kz + 1) % groups})
    pl.semaphore_signal(barrier, 1, device_id={"kz": (kz + groups - 1) % groups})

    out[...] = jnp.zeros_like(out)
    part_out[...] = jnp.zeros_like(part_out)

    for copy in smalls[:2]:
        copy.wait()
    match[...] = (angle[...] == lax.broadcasted_iota(I32, (angles, spokes), 0)).astype(F32)
    for copy in smalls[2:]:
        copy.wait()
    for cut in range(2, CUTS):
        interp_copy(cut).start()
    for batch in range(1, batches):
        data_copy(batch).start()
    across = side // seg
    row = lax.broadcasted_iota(I32, (side, hits), 0) * across
    hit_at = jnp.concatenate([where[g : g + 1, :] for g in range(segs)], axis=1)
    for h in range(across):
        here = (hit_at == row + h).astype(F32).astype(BF16)
        for r in range(2):
            part = jnp.dot(dft[r], here, preferred_element_type=F32)
            if r == 0:
                ymat[h, :side, :hits] = part.astype(BF16)
                ymat[h, side:, hits:] = part.astype(BF16)
            else:
                ymat[h, :side, hits:] = part.astype(BF16)
                ymat[h, side:, :hits] = (-part).astype(BF16)
    cos_x, sin_x = dft[0], dft[1]
    xmat[:side, :side] = cos_x
    xmat[:side, side:] = -sin_x
    xmat[side:, :side] = sin_x
    xmat[side:, side:] = cos_x

    def kept_start(order, stage):
        start = 0
        for s in range(stage):
            start = start + my_bit[order[s]] * (blocks >> (s + 1))
        return start

    half = blocks // 2

    def first_copy(step, span, arrived):
        chunk = pl.ds(step * lanes, lanes)
        return pltpu.make_async_remote_copy(
            src_ref=weighted.at[chunk, pl.ds((1 - my_bit[0]) * half, half), span],
            dst_ref=inbox[0].at[chunk, :, span],
            send_sem=sent.at[0],
            recv_sem=first_recv.at[arrived, step],
            device_id={"coil": partner[0]},
        )

    def first_of_pair(pair, step):
        return first_copy(step, pl.ds(pair * SUB, SUB), pair // per_batch)

    def first_of_batch(batch, step):
        return first_copy(step, of(batch), batch)

    def all_first():
        return pltpu.make_async_remote_copy(
            src_ref=weighted.at[:, pl.ds(0, half)],
            dst_ref=inbox[0],
            send_sem=sent.at[0],
            recv_sem=first_recv.at[0, 0],
            device_id={"coil": partner[0]},
        )

    def of(batch):
        return pl.ds(batch * share, share)

    def half_copy(batch, step, lane, stage):
        order = orders[lane % 2]
        bit = order[stage]
        size = blocks >> (stage + 1)
        start = kept_start(order, stage) + (1 - my_bit[bit]) * size
        chunk = step * lanes + lane
        return pltpu.make_async_remote_copy(
            src_ref=weighted.at[chunk, pl.ds(start, size), of(batch)],
            dst_ref=inbox[stage].at[chunk, :, of(batch)],
            send_sem=sent.at[stage],
            recv_sem=half_recv.at[stage - 1, batch, step],
            device_id={"coil": partner[bit]},
        )

    def half_of_step(batch, step, stage):
        size = blocks >> (stage + 1)
        chunk = pl.ds(step * lanes, lanes)
        return pltpu.make_async_remote_copy(
            src_ref=weighted.at[chunk, pl.ds(0, size), of(batch)],
            dst_ref=inbox[stage].at[chunk, :, of(batch)],
            send_sem=sent.at[stage],
            recv_sem=half_recv.at[stage - 1, batch, step],
            device_id={"coil": partner[stage]},
        )

    def all_half(stage):
        return pltpu.make_async_remote_copy(
            src_ref=weighted.at[:, pl.ds(0, blocks >> (stage + 1))],
            dst_ref=inbox[stage],
            send_sem=sent.at[stage],
            recv_sem=half_recv.at[stage - 1, 0, 0],
            device_id={"coil": partner[stage]},
        )

    def add_inbox(batch, step, lane, stage):
        size = blocks >> (stage + 1)
        start = kept_start(orders[lane % 2], stage + 1)
        chunk = step * lanes + lane
        for b in range(size):
            total = weighted[chunk, start + b, of(batch)] + inbox[stage][chunk, b, of(batch)]
            if stage < bits - 1:
                weighted[chunk, start + b, of(batch)] = total
            else:
                raw[step, kz, lane, of(batch)] = total

    def raw_copy(batch, step, source, leaves, lands):
        return pltpu.make_async_remote_copy(
            src_ref=raw.at[step, source, :, of(batch)],
            dst_ref=raw.at[step, source, :, of(batch)],
            send_sem=sent.at[bits + leaves],
            recv_sem=line_recv.at[lands, batch, step],
            device_id={"kz": inward},
        )

    def from_outer(batch, step, source):
        return raw_copy(batch, step, source, 0, 0)

    def from_inner(batch, step, source):
        return raw_copy(batch, step, source, 0, 1)

    def forward(batch, step, source):
        return raw_copy(batch, step, source, 1, 1)

    def far_side(batch, step):
        return raw_copy(batch, step, pl.ds(jnp.where(kz < 2, 2, 0), 2), 0, 1)

    def all_raw(source, leaves):
        return pltpu.make_async_remote_copy(
            src_ref=raw.at[:, source],
            dst_ref=raw.at[:, source],
            send_sem=sent.at[bits + leaves],
            recv_sem=line_recv.at[0, 0, 0],
            device_id={"kz": inward},
        )

    def partial(step, lane):
        return pltpu.make_async_remote_copy(
            src_ref=part_out.at[step, lane],
            dst_ref=part_in.at[step, lane],
            send_sem=sent.at[bits + 2],
            recv_sem=line_recv.at[0, lane, step],
            device_id={"kz": outward},
        )

    def all_partial():
        return pltpu.make_async_remote_copy(
            src_ref=part_out,
            dst_ref=part_in,
            send_sem=sent.at[bits + 2],
            recv_sem=line_recv.at[0, 0, 0],
            device_id={"kz": outward},
        )

    def bin_batch(batch):
        data_copy(batch).wait()
        spot = lax.broadcasted_iota(I32, (angles, spokes), 1)
        for i in range(share):
            p = batch * share + i
            weights = jnp.where(spot < count[p], match[...], 0.0).astype(BF16)
            for r in range(2):
                total = jnp.dot(weights, kdata[r, p], preferred_element_type=F32)
                for g in range(segs):
                    binned[g, pl.ds(i * 2 + r, angles, stride=SUBLANE), :] = total[:, g * seg : (g + 1) * seg]

    def interpolate(batch, cut):
        @pl.when(batch == 0)
        def _():
            interp_copy(cut).wait()

        empty = jnp.zeros((2 * SUBLANE, seg), BF16)
        for pair in range(per_cut // 2):
            a = cut * per_cut + pair * 2
            rows_at = pl.ds(pl.multiple_of(a * SUBLANE, 2 * SUBLANE), 2 * SUBLANE)
            for g in range(0, segs, 2):
                low, high = [binned[g + i, rows_at, :].astype(BF16) for i in range(2)]
                rows_in = jnp.concatenate(
                    [jnp.concatenate([low, empty], axis=1), jnp.concatenate([empty, high], axis=1)], axis=0
                )
                matrix = jnp.concatenate(
                    [jnp.concatenate([interp[a, g + i], interp[a + 1, g + i]], axis=1) for i in range(2)], axis=0
                )
                both = jnp.dot(rows_in, matrix, preferred_element_type=F32)
                for i in range(2):
                    for j in range(2):
                        top = (2 * i + j) * SUBLANE
                        hit = (g + i) * angles + a + j
                        contrib[batch, pl.ds(hit, SUBLANE, stride=pitch), :] = both[top : top + SUBLANE, j * seg : (j + 1) * seg]

    def compute(pair):
        first = pair * SUB
        batch = pair // per_batch
        at = (pair % per_batch) * SUB

        def column(s):
            tops = [pl.multiple_of(((at + s) * 2 + r) * pitch, SUBLANE) for r in range(2)]
            return jnp.concatenate([contrib[batch, pl.ds(top, hits), :] for top in tops], axis=0).astype(BF16)

        data = jnp.concatenate([column(s) for s in range(SUB)], axis=1)
        halves = [jnp.dot(ymat[h], data, preferred_element_type=F32).astype(BF16) for h in range(across)]
        s_re = sens[0].astype(F32)
        s_im = sens[1].astype(F32)
        for s in range(SUB):
            pieces = [h[r * side : (r + 1) * side, s * seg : (s + 1) * seg] for r in range(2) for h in halves]
            image = jnp.dot(jnp.concatenate(pieces, axis=1), xmat[...], preferred_element_type=F32)
            i_re, i_im = image[:, :side], image[:, side:]
            result = [s_re * i_re + s_im * i_im, s_re * i_im - s_im * i_re]
            for block in range(blocks):
                for lane in range(lanes):
                    place = 0
                    for bit in orders[lane % 2]:
                        place = place * 2 + (block >> bit) % 2
                    for step in range(steps):
                        top = block * rows + step * SUBLANE
                        for r in range(2):
                            weighted[step * lanes + lane, place, first + s, r] = result[r][
                                top : top + SUBLANE, lane * LANE : (lane + 1) * LANE
                            ]

    def transform(batch, step, lane, sources, owner, load, store):
        for q in range(groups):
            sums = []
            for i in range(share):
                re = im = None
                for j in sources:
                    turn = 2.0 * math.pi * (q * j % groups) / groups
                    c, d = round(math.cos(turn), 12), round(math.sin(turn), 12)
                    k = batch * share + i
                    x_re, x_im = raw[step, j, lane, k, 0], raw[step, j, lane, k, 1]
                    for coef, a, b in ((c, x_re, x_im), (d, x_im, -x_re)):
                        if coef == 0.0:
                            continue
                        ta = a if coef == 1.0 else a * F32(coef)
                        tb = b if coef == 1.0 else b * F32(coef)
                        re = ta if re is None else re + ta
                        im = tb if im is None else im + tb
                sums.append((re, im))
            for z in range(q, parts, groups):
                a_re, a_im = load(z)
                for i in range(share):
                    spot = (owner * parts + batch * share + i) * 2 * parts + z
                    c, d = twiddle[spot], twiddle[spot + parts]
                    re, im = sums[i]
                    a_re = a_re + (c * re + d * im)
                    a_im = a_im + (c * im - d * re)
                store(z, a_re, a_im)

    def spot(step, lane):
        return pl.ds(pl.multiple_of(step * SUBLANE, SUBLANE), SUBLANE), pl.ds(lane * LANE, LANE)

    def in_out(step, lane):
        y, x = spot(step, lane)

        def load(z):
            return out[0, z, y, x], out[1, z, y, x]

        def store(z, re, im):
            out[0, z, y, x] = re
            out[1, z, y, x] = im

        return load, store

    def in_partial(step, lane):
        def load(z):
            return part_out[step, lane, z, 0], part_out[step, lane, z, 1]

        def store(z, re, im):
            part_out[step, lane, z, 0] = re
            part_out[step, lane, z, 1] = im

        return load, store

    def reduce_stage(stage, batch, step):
        if stage == 0:
            first_of_batch(batch, step).wait_recv()
        else:
            half_of_step(batch, step, stage).wait_recv()

        for lane in range(lanes):
            add_inbox(batch, step, lane, stage)
            if stage < bits - 1:
                half_copy(batch, step, lane, stage + 1).start()
        if stage == bits - 1:

            @pl.when(outer)
            def _():
                from_outer(batch, step, kz).start()

            @pl.when(inner)
            def _():
                from_inner(batch, step, kz).start()

    def relay_stage(batch, step):
        @pl.when(inner)
        def _():
            from_outer(batch, step, outward).wait_recv()
            forward(batch, step, outward).start()

        for end in (0, last):

            @pl.when(kz == end)
            def _(end=end):
                for lane in range(lanes):
                    transform(batch, step, lane, [end], kz, *in_out(step, lane))

    def combine_stage(batch, step):
        @pl.when(inner)
        def _():
            far_side(batch, step).wait_recv()

        for place, end in ((1, 0), (last - 1, last)):

            @pl.when(kz == place)
            def _(end=end):
                for lane in range(lanes):
                    transform(batch, step, lane, [j for j in range(groups) if j != end], outward, *in_partial(step, lane))

                    @pl.when(batch == batches - 1)
                    def _():
                        partial(step, lane).start()

        @pl.when(inner)
        def _():
            for lane in range(lanes):
                transform(batch, step, lane, list(range(groups)), kz, *in_out(step, lane))

            @pl.when(batch == batches - 1)
            def _():
                out_copy(step).start()

    def out_copy(step):
        y = pl.ds(step * SUBLANE, SUBLANE)
        return pltpu.make_async_copy(out.at[:, :, y], out_hbm.at[:, :, y], out_sem.at[0])

    def finish(step):
        @pl.when(outer)
        def _():
            for lane in range(lanes):
                partial(step, lane).wait_recv()
                y, x = spot(step, lane)
                for r in range(2):
                    out[r, :, y, x] = out[r, :, y, x] + part_in[step, lane, :, r]
            out_copy(step).start()

    bins, cuts, pair_at, items, starts = plan(steps, batches, per_batch)

    def pick(t, table):
        value = 0
        for key, entry in table.items():
            value = value + jnp.where(t == key, entry, 0)
        return value

    def tick(t, carry):
        def at(lag, body):
            when = [start + lag for start in starts]
            found = pick(t, {k: 1 for k in when})
            batch = pick(t, {k: item[0] for k, item in zip(when, items)})
            step = pick(t, {k: item[1] for k, item in zip(when, items)})

            @pl.when(found > 0)
            def _():
                body(batch, step)

        at(LAG * bits, relay_stage)
        for stage in range(bits - 1, -1, -1):
            at(LAG * stage, functools.partial(reduce_stage, stage))

        @pl.when(pick(t, {k: 1 for k in bins}) > 0)
        def _():
            bin_batch(pick(t, bins))

        batch, low, high = [pick(t, {k: v[i] for k, v in cuts.items()}) for i in range(3)]

        def one_cut(cut, carry):
            interpolate(batch, cut)
            return carry

        lax.fori_loop(low, high, one_cut, 0)
        first, end = [pick(t, {k: v[i] for k, v in pair_at.items()}) for i in range(2)]

        def one_pair(pair, carry):
            compute(pair)
            for step in range(steps):
                first_of_pair(pair, step).start()
            return carry

        lax.fori_loop(first, end, one_pair, 0)
        at(LAG * bits + LAG, combine_stage)
        return carry

    pl.semaphore_wait(barrier, bits + 2)
    lax.fori_loop(0, starts[-1] + LAG * bits + LAG + 1, tick, 0)

    def finish_early(step, carry):
        finish(step)
        return carry

    lax.fori_loop(0, steps - 1, finish_early, 0)

    all_first().wait_send()
    for stage in range(1, bits):
        all_half(stage).wait_send()
    all_raw(kz, 0).wait_send()
    finish(steps - 1)

    @pl.when(inner)
    def _():
        all_raw(outward, 1).wait_send()
        all_partial().wait_send()

    pltpu.make_async_copy(out, out_hbm, out_sem.at[0]).wait()


def per_device(kdata, spoke_angle, spoke_count, block_index, interp, sens_maps):
    side = sens_maps.shape[2]
    parts = kdata.shape[1]
    spokes, samples = kdata.shape[3:]
    angles, segs, seg = interp.shape[:3]
    coils = lax.axis_size("coil")
    groups = lax.axis_size("kz")
    bits = coils.bit_length() - 1
    rows = side // coils
    hits = angles * segs
    share = SUBLANE // 2
    batches = parts // share
    steps = rows // SUBLANE
    lanes = side // LANE
    across = side // seg

    assert groups == 4 and parts % groups == 0 and parts % share == 0 and angles % (2 * CUTS) == 0 and segs % 2 == 0
    index = np.arange(side)
    dft = jnp.asarray(np.stack(cos_sin(index[:, None] * index[None, :], side)), BF16)
    low = np.arange(parts)
    tables = []
    for owner in range(groups):
        pair = cos_sin(low[:, None] * (owner * parts + low)[None, :], parts * groups)
        tables.append(np.stack(pair, 1))
    twiddle = jnp.asarray(np.stack(tables).reshape(-1), F32)

    chunks = steps * lanes
    block = (parts, 2, SUBLANE, LANE)
    vmem = pltpu.VMEM
    scratch = [
        vmem((2, parts, spokes, samples), BF16),
        vmem((1, spokes), I32),
        pltpu.SMEM((parts,), I32),
        vmem((segs, angles), I32),
        vmem((angles, segs, seg, seg), BF16),
        vmem((2, side, side), BF16),
        vmem((2, side, side), BF16),
        pltpu.SMEM(twiddle.shape, F32),
        vmem((across, 2 * side, 2 * hits), BF16),
        vmem((2 * side, 2 * side), BF16),
        vmem((angles, spokes), F32),
        vmem((segs, angles * SUBLANE, seg), F32),
        vmem((batches, 2 * share * (hits + SUBLANE), seg), F32),
        vmem((chunks, coils) + block, F32),
        vmem((steps, groups, lanes) + block, F32),
        vmem((steps, lanes) + block, F32),
        vmem((steps, lanes) + block, F32),
    ]
    scratch += [vmem((chunks, coils >> (s + 1)) + block, F32) for s in range(bits)]
    dma = pltpu.SemaphoreType.DMA
    scratch += [vmem((2, parts, rows, side), F32)]
    scratch += [dma((6,)), dma((batches,)), dma((CUTS,)), dma((1,))]
    scratch += [dma((bits + 3,)), dma((batches, steps)), dma((bits - 1, batches, steps)), dma((2, batches, steps))]
    anywhere = pl.BlockSpec(memory_space=pltpu.HBM)
    dims = (bits, groups, parts, rows, side, angles, segs, seg, spokes)
    return pl.pallas_call(
        functools.partial(kernel, dims),
        out_shape=jax.ShapeDtypeStruct((2, parts, rows, side), F32),
        in_specs=[anywhere] * 8,
        out_specs=anywhere,
        scratch_shapes=scratch,
        compiler_params=pltpu.CompilerParams(
            collective_id=0, has_side_effects=True, vmem_limit_bytes=60 * 1024 * 1024
        ),
        name="reconstruct",
    )(
        kdata[:, :, 0],
        spoke_angle.reshape(1, -1),
        spoke_count,
        block_index.T,
        interp,
        sens_maps[:, 0],
        dft,
        twiddle,
    )


def solution(mesh):
    placed = (
        P(None, "kz", "coil", None, None),
        P(),
        P("kz"),
        P(),
        P(),
        P(None, "coil", None, None),
    )
    return jax.shard_map(
        per_device,
        mesh=mesh,
        in_specs=placed,
        out_specs=P(None, "kz", "coil", None),
        check_vma=False,
    )
```

time: 107 us -> 80.1 us (0.75)
  matrix products: 11.2 us -> 0 us
  other arithmetic: 7.27 us -> 0 us
  local copies, waits for them, and re-layouts: 7.02 us -> 2.31 us
  Pallas kernels: 81.2 us -> 77.6 us
    dot_general x2 -> x0, matrix products: 11.2 us -> none  [the longest x1 6.31 us: per_device(): jnp.einsum('rpagj,agjt->pragt', pieces, interp, preferred_element_type=F32)]
    pallas_call x1, Pallas kernels: 81.2 us -> 77.6 us  [per_device(): pl.pallas_call(functools.partial(kernel, dims), out_shape=jax.ShapeDtypeS...]
    another operation x4 -> x0, other arithmetic: 2.8 us -> none
    convert_element_type x1 -> x0, local copies, waits for them, and re-layouts: 2.43 us -> none  [per_device(): jnp.einsum('rpagj,agjt->pragt', pieces, interp, preferred_element_type=F32)]
    reshape x2 -> x0, local copies, waits for them, and re-layouts: 2.18 us -> none  [the longest x1 2.07 us: per_device(): pieces = binned.reshape(2, parts, angles, segs, seg)]
    concatenate x2 -> x0, other arithmetic: 1.88 us -> none  [the longest x1 1.05 us: per_device(): jnp.concatenate([jnp.concatenate([cos_y, sin_y], 2), jnp.concatenate([-si...]
    mul x2 -> x0, other arithmetic: 1.14 us -> none  [the longest x1 1.05 us: cos_sin(): jnp.sin(phase) * scale]
    unnamed x4 -> x1, local copies, waits for them, and re-layouts: 2.41 us -> 2.31 us
where the time goes in v1:
time: 80.1 us; the launch traced here: 79.9 us
  Pallas kernels  77.6 us (97%)
  local copies, waits for them, and re-layouts  2.31 us (3%)
    pallas_call x1, Pallas kernels, per_device(): pl.pallas_call(functools.partial(kernel, dims), out_shape=jax.ShapeDtypeS...  77.6 us
    unnamed x1, local copies, waits for them, and re-layouts  2.31 us

profile of v1, /device:TPU:0, one launch (start us, length us, event | category | flops | bytes accessed | tf_op | source)
XLA Modules:
  0.0 79.9 jit_solution(7638812446518078465)
XLA Ops:
  0.0 77.6 %reconstruct.1 = f32[2,16,32,256]{3,2,1,0:T(8,128)} custom-call(bf16[2,16,256,512]{3,2,1,0:T(8,128)(2,1)} %bitcast.4, s32[1,256]{1,0:T(1,128)} %bitcast.7, s32[16]{0:T(128)} %refs_2_.1, s32[4,64]{1,0:T(4,128)} %bitcast.6, bf16[64,4,128,128]{3,2,1,0:T(8,128)(2,1)} %refs_4_.1, bf16[2,256,256]{2,1,0:T(8,128)(2,1)} %bitcast.5, ...), custom_call_target="tpu_custom_call" | custom-call | tf_op jit(solution)/shard_map/reconstruct/pallas_call | solution.py:580
  77.6 2.3 %copy.10 = f32[2,16,32,256]{3,2,1,0:T(8,128)} copy(f32[2,16,32,256]{3,2,1,0:T(8,128)} %reconstruct.1) | data formatting | bytes 2097152

commit v2 on v1

--- a/solution.py
+++ b/solution.py
@@ -15,7 +15,7 @@
 SUB = 2
 SUBLANE, LANE = 8, 128
 CUTS = 4
-LAG = 2
+LAG = 3
 
 
 def cos_sin(product, length):
@@ -29,34 +29,45 @@
     return [first, first[:1] + first[:0:-1]]
 
 
-def plan(steps, batches, per_batch):
-    if steps == 4 and batches == 4 and per_batch == 2:
-        half = CUTS // 2
-        bins = {0: 0, 4: 1, 7: 2, 9: 3}
-        cuts = {0: (0, 0, CUTS), 4: (1, 0, CUTS), 7: (2, 0, half), 8: (2, half, CUTS), 10: (3, 0, CUTS)}
-        pairs = {1: (0, 1), 2: (1, 2), 5: (2, 3), 6: (3, 4), 8: (4, 5), 9: (5, 6), 11: (6, 8)}
-        items = [(0, s) for s in range(4)] + [(1 + k // 2, k % 2) for k in range(6)] + [(1 + k % 3, 2 + k // 3) for k in range(6)]
-        return bins, cuts, pairs, items, [k + 3 if k < 4 else k + 4 for k in range(16)]
-    items = [(b, s) for b in range(batches) for s in range(steps)]
+def plan(chunks, batches, per_batch):
+    if chunks == 8 and batches == 4 and per_batch == 2 and CUTS == 4:
+        bins = {0: 0, 4: 1, 9: 2, 14: 3}
+        cuts = {0: (0, 0, 4)}
+        for b, t in ((1, 4), (2, 9), (3, 14)):
+            cuts |= {t: (b, 0, 1), t + 1: (b, 1, 3), t + 2: (b, 3, 4)}
+        pairs = {1: (0, 1), 2: (1, 2), 7: (2, 3), 8: (3, 4), 11: (4, 5), 12: (5, 6), 16: (6, 7), 17: (7, 8)}
+        return bins, cuts, pairs, 3, True
     bins = {2 * b: b for b in range(batches)}
     cuts = {2 * b: (b, 0, CUTS) for b in range(batches)}
     pairs = {2 * b + 1: (b * per_batch, (b + 1) * per_batch) for b in range(batches)}
-    return bins, cuts, pairs, items, [2 * batches + k for k in range(len(items))]
+    return bins, cuts, pairs, 2 * batches, False
+
+
+def nth_item(k, chunks, mixed):
+    if not mixed:
+        return lax.div(k, chunks), lax.rem(k, chunks)
+    a, b, c = [jnp.maximum(k, first) - first for first in (8, 20, 26)]
+    late_batch = jnp.where(k < 26, 1 + lax.div(b, 2), 1 + lax.rem(c, 3))
+    late_chunk = jnp.where(k < 26, 4 + lax.rem(b, 2), 6 + lax.div(c, 3))
+    batch = jnp.where(k < 8, 0, jnp.where(k < 20, 1 + lax.div(a, 4), late_batch))
+    chunk = jnp.where(k < 8, k, jnp.where(k < 20, lax.rem(a, 4), late_chunk))
+    return batch, chunk
 
 
 def kernel(dims, *refs):
     bits, groups, parts, rows, side, angles, segs, seg, spokes = dims
-    kdata_in, angle_in, count_in, where_in, interp_in, sens_in, dft_in, twiddle_in, out_hbm = refs[:9]
+    kdata_in, angle_in, count_in, where_in, interp_in, sens_in, dft_in, twiddle_in, out = refs[:9]
     kdata, angle, count, where, interp, sens, dft, twiddle = refs[9:17]
     ymat, xmat, match, binned, contrib = refs[17:22]
     weighted, raw, part_out, part_in = refs[22:26]
     inbox = refs[26 : 26 + bits]
-    out, small_sem, data_sem, interp_sem, out_sem = refs[26 + bits : 31 + bits]
-    sent, first_recv, half_recv, line_recv = refs[31 + bits :]
+    small_sem, data_sem, interp_sem = refs[26 + bits : 29 + bits]
+    sent, first_recv, half_recv, line_recv = refs[29 + bits :]
     blocks = 1 << bits
     orders = halving_orders(bits)
     lanes = side // LANE
     steps = rows // SUBLANE
+    chunks = steps * lanes
     share = SUBLANE // 2
     batches = parts // share
     per_batch = share // SUB
@@ -142,18 +153,21 @@
 
     half = blocks // 2
 
+    def of(batch):
+        return pl.ds(batch * per_batch, per_batch)
+
     def first_copy(step, span, arrived):
         chunk = pl.ds(step * lanes, lanes)
         return pltpu.make_async_remote_copy(
-            src_ref=weighted.at[chunk, pl.ds((1 - my_bit[0]) * half, half), span],
-            dst_ref=inbox[0].at[chunk, :, span],
+            src_ref=weighted.at[chunk, pl.ds((1 - my_bit[0]) * half, half), :, span],
+            dst_ref=inbox[0].at[chunk, :, :, span],
             send_sem=sent.at[0],
             recv_sem=first_recv.at[arrived, step],
             device_id={"coil": partner[0]},
         )
 
     def first_of_pair(pair, step):
-        return first_copy(step, pl.ds(pair * SUB, SUB), pair // per_batch)
+        return first_copy(step, pl.ds(pair, 1), pair // per_batch)
 
     def first_of_batch(batch, step):
         return first_copy(step, of(batch), batch)
@@ -167,31 +181,25 @@
             device_id={"coil": partner[0]},
         )
 
-    def of(batch):
-        return pl.ds(batch * share, share)
-
-    def half_copy(batch, step, lane, stage):
-        order = orders[lane % 2]
+    def half_copy(batch, chunk, way, stage):
+        order = orders[way]
         bit = order[stage]
         size = blocks >> (stage + 1)
         start = kept_start(order, stage) + (1 - my_bit[bit]) * size
-        chunk = step * lanes + lane
-        return pltpu.make_async_remote_copy(
-            src_ref=weighted.at[chunk, pl.ds(start, size), of(batch)],
-            dst_ref=inbox[stage].at[chunk, :, of(batch)],
+        return pltpu.make_async_remote_copy(
+            src_ref=weighted.at[chunk, pl.ds(start, size), way, of(batch)],
+            dst_ref=inbox[stage].at[chunk, :, way, of(batch)],
             send_sem=sent.at[stage],
-            recv_sem=half_recv.at[stage - 1, batch, step],
+            recv_sem=half_recv.at[stage - 1, batch, chunk],
             device_id={"coil": partner[bit]},
         )
 
-    def half_of_step(batch, step, stage):
-        size = blocks >> (stage + 1)
-        chunk = pl.ds(step * lanes, lanes)
-        return pltpu.make_async_remote_copy(
-            src_ref=weighted.at[chunk, pl.ds(0, size), of(batch)],
-            dst_ref=inbox[stage].at[chunk, :, of(batch)],
+    def both_halves(batch, chunk, stage):
+        return pltpu.make_async_remote_copy(
+            src_ref=weighted.at[chunk, pl.ds(0, blocks >> (stage + 1)), :, of(batch)],
+            dst_ref=inbox[stage].at[chunk, :, :, of(batch)],
             send_sem=sent.at[stage],
-            recv_sem=half_recv.at[stage - 1, batch, step],
+            recv_sem=half_recv.at[stage - 1, batch, chunk],
             device_id={"coil": partner[stage]},
         )
 
@@ -204,37 +212,43 @@
             device_id={"coil": partner[stage]},
         )
 
-    def add_inbox(batch, step, lane, stage):
+    def add_inbox(batch, chunk, way, stage):
         size = blocks >> (stage + 1)
-        start = kept_start(orders[lane % 2], stage + 1)
-        chunk = step * lanes + lane
+        start = kept_start(orders[way], stage + 1)
         for b in range(size):
-            total = weighted[chunk, start + b, of(batch)] + inbox[stage][chunk, b, of(batch)]
+            total = weighted[chunk, start + b, way, of(batch)] + inbox[stage][chunk, b, way, of(batch)]
             if stage < bits - 1:
-                weighted[chunk, start + b, of(batch)] = total
+                weighted[chunk, start + b, way, of(batch)] = total
             else:
-                raw[step, kz, lane, of(batch)] = total
-
-    def raw_copy(batch, step, source, leaves, lands):
-        return pltpu.make_async_remote_copy(
-            src_ref=raw.at[step, source, :, of(batch)],
-            dst_ref=raw.at[step, source, :, of(batch)],
+                raw[chunk, kz, way, of(batch)] = total
+
+    def raw_copy(batch, chunk, source, leaves, lands):
+        return pltpu.make_async_remote_copy(
+            src_ref=raw.at[chunk, source, :, of(batch)],
+            dst_ref=raw.at[chunk, source, :, of(batch)],
             send_sem=sent.at[bits + leaves],
-            recv_sem=line_recv.at[lands, batch, step],
+            recv_sem=line_recv.at[lands, batch, chunk],
             device_id={"kz": inward},
         )
 
-    def from_outer(batch, step, source):
-        return raw_copy(batch, step, source, 0, 0)
-
-    def from_inner(batch, step, source):
-        return raw_copy(batch, step, source, 0, 1)
-
-    def forward(batch, step, source):
-        return raw_copy(batch, step, source, 1, 1)
-
-    def far_side(batch, step):
-        return raw_copy(batch, step, pl.ds(jnp.where(kz < 2, 2, 0), 2), 0, 1)
+    def from_outer(batch, chunk, source):
+        return raw_copy(batch, chunk, source, 0, 0)
+
+    def from_inner(batch, chunk, source):
+        return raw_copy(batch, chunk, source, 0, 1)
+
+    def forward(batch, chunk, source):
+        return raw_copy(batch, chunk, source, 1, 1)
+
+    def far_side(batch, chunk):
+        far = pl.ds(jnp.where(kz < 2, 2, 0), 2)
+        return pltpu.make_async_remote_copy(
+            src_ref=raw.at[chunk, far, :, of(batch)],
+            dst_ref=raw.at[chunk, far, :, of(batch)],
+            send_sem=sent.at[bits],
+            recv_sem=line_recv.at[1, batch, chunk],
+            device_id={"kz": inward},
+        )
 
     def all_raw(source, leaves):
         return pltpu.make_async_remote_copy(
@@ -245,12 +259,12 @@
             device_id={"kz": inward},
         )
 
-    def partial(step, lane):
-        return pltpu.make_async_remote_copy(
-            src_ref=part_out.at[step, lane],
-            dst_ref=part_in.at[step, lane],
+    def partial(chunk):
+        return pltpu.make_async_remote_copy(
+            src_ref=part_out.at[chunk],
+            dst_ref=part_in.at[chunk],
             send_sem=sent.at[bits + 2],
-            recv_sem=line_recv.at[0, lane, step],
+            recv_sem=line_recv.at[0, 0, chunk],
             device_id={"kz": outward},
         )
 
@@ -299,7 +313,6 @@
                         contrib[batch, pl.ds(hit, SUBLANE, stride=pitch), :] = both[top : top + SUBLANE, j * seg : (j + 1) * seg]
 
     def compute(pair):
-        first = pair * SUB
         batch = pair // per_batch
         at = (pair % per_batch) * SUB
 
@@ -317,18 +330,18 @@
             i_re, i_im = image[:, :side], image[:, side:]
             result = [s_re * i_re + s_im * i_im, s_re * i_im - s_im * i_re]
             for block in range(blocks):
+                place = 0
+                for bit in orders[s % 2]:
+                    place = place * 2 + (block >> bit) % 2
                 for lane in range(lanes):
-                    place = 0
-                    for bit in orders[lane % 2]:
-                        place = place * 2 + (block >> bit) % 2
                     for step in range(steps):
                         top = block * rows + step * SUBLANE
                         for r in range(2):
-                            weighted[step * lanes + lane, place, first + s, r] = result[r][
+                            weighted[step * lanes + lane, place, s, pair, r] = result[r][
                                 top : top + SUBLANE, lane * LANE : (lane + 1) * LANE
                             ]
 
-    def transform(batch, step, lane, sources, owner, load, store):
+    def transform(batch, chunk, sources, owner, load, store):
         for q in range(groups):
             sums = []
             for i in range(share):
@@ -336,8 +349,7 @@
                 for j in sources:
                     turn = 2.0 * math.pi * (q * j % groups) / groups
                     c, d = round(math.cos(turn), 12), round(math.sin(turn), 12)
-                    k = batch * share + i
-                    x_re, x_im = raw[step, j, lane, k, 0], raw[step, j, lane, k, 1]
+                    x_re, x_im = [raw[chunk, j, i % SUB, batch * per_batch + i // SUB, r] for r in range(2)]
                     for coef, a, b in ((c, x_re, x_im), (d, x_im, -x_re)):
                         if coef == 0.0:
                             continue
@@ -356,11 +368,13 @@
                     a_im = a_im + (c * im - d * re)
                 store(z, a_re, a_im)
 
-    def spot(step, lane):
-        return pl.ds(pl.multiple_of(step * SUBLANE, SUBLANE), SUBLANE), pl.ds(lane * LANE, LANE)
-
-    def in_out(step, lane):
-        y, x = spot(step, lane)
+    def spot(chunk):
+        y = pl.multiple_of(lax.div(chunk, lanes) * SUBLANE, SUBLANE)
+        x = pl.multiple_of(lax.rem(chunk, lanes) * LANE, LANE)
+        return pl.ds(y, SUBLANE), pl.ds(x, LANE)
+
+    def in_out(chunk):
+        y, x = spot(chunk)
 
         def load(z):
             return out[0, z, y, x], out[1, z, y, x]
@@ -371,89 +385,79 @@
 
         return load, store
 
-    def in_partial(step, lane):
+    def in_partial(chunk):
         def load(z):
-            return part_out[step, lane, z, 0], part_out[step, lane, z, 1]
+            return part_out[chunk, z, 0], part_out[chunk, z, 1]
 
         def store(z, re, im):
-            part_out[step, lane, z, 0] = re
-            part_out[step, lane, z, 1] = im
+            part_out[chunk, z, 0] = re
+            part_out[chunk, z, 1] = im
 
         return load, store
 
-    def reduce_stage(stage, batch, step):
+    def reduce_stage(stage, batch, chunk):
         if stage == 0:
-            first_of_batch(batch, step).wait_recv()
+
+            @pl.when(lax.rem(chunk, lanes) == 0)
+            def _():
+                first_of_batch(batch, lax.div(chunk, lanes)).wait_recv()
         else:
-            half_of_step(batch, step, stage).wait_recv()
-
-        for lane in range(lanes):
-            add_inbox(batch, step, lane, stage)
+            both_halves(batch, chunk, stage).wait_recv()
+        for way in range(2):
+            add_inbox(batch, chunk, way, stage)
             if stage < bits - 1:
-                half_copy(batch, step, lane, stage + 1).start()
+                half_copy(batch, chunk, way, stage + 1).start()
         if stage == bits - 1:
 
             @pl.when(outer)
             def _():
-                from_outer(batch, step, kz).start()
+                from_outer(batch, chunk, kz).start()
 
             @pl.when(inner)
             def _():
-                from_inner(batch, step, kz).start()
-
-    def relay_stage(batch, step):
+                from_inner(batch, chunk, kz).start()
+
+    def relay_stage(batch, chunk):
         @pl.when(inner)
         def _():
-            from_outer(batch, step, outward).wait_recv()
-            forward(batch, step, outward).start()
+            from_outer(batch, chunk, outward).wait_recv()
+            forward(batch, chunk, outward).start()
 
         for end in (0, last):
 
             @pl.when(kz == end)
             def _(end=end):
-                for lane in range(lanes):
-                    transform(batch, step, lane, [end], kz, *in_out(step, lane))
-
-    def combine_stage(batch, step):
+                transform(batch, chunk, [end], kz, *in_out(chunk))
+
+    def combine_stage(batch, chunk):
         @pl.when(inner)
         def _():
-            far_side(batch, step).wait_recv()
+            far_side(batch, chunk).wait_recv()
 
         for place, end in ((1, 0), (last - 1, last)):
 
             @pl.when(kz == place)
             def _(end=end):
-                for lane in range(lanes):
-                    transform(batch, step, lane, [j for j in range(groups) if j != end], outward, *in_partial(step, lane))
-
-                    @pl.when(batch == batches - 1)
-                    def _():
-                        partial(step, lane).start()
+                transform(batch, chunk, [j for j in range(groups) if j != end], outward, *in_partial(chunk))
+
+                @pl.when(batch == batches - 1)
+                def _():
+                    partial(chunk).start()
 
         @pl.when(inner)
         def _():
-            for lane in range(lanes):
-                transform(batch, step, lane, list(range(groups)), kz, *in_out(step, lane))
-
-            @pl.when(batch == batches - 1)
-            def _():
-                out_copy(step).start()
-
-    def out_copy(step):
-        y = pl.ds(step * SUBLANE, SUBLANE)
-        return pltpu.make_async_copy(out.at[:, :, y], out_hbm.at[:, :, y], out_sem.at[0])
-
-    def finish(step):
+            transform(batch, chunk, list(range(groups)), kz, *in_out(chunk))
+
+    def finish(chunk):
         @pl.when(outer)
         def _():
-            for lane in range(lanes):
-                partial(step, lane).wait_recv()
-                y, x = spot(step, lane)
-                for r in range(2):
-                    out[r, :, y, x] = out[r, :, y, x] + part_in[step, lane, :, r]
-            out_copy(step).start()
-
-    bins, cuts, pair_at, items, starts = plan(steps, batches, per_batch)
+            partial(chunk).wait_recv()
+            y, x = spot(chunk)
+            for r in range(2):
+                out[r, :, y, x] = out[r, :, y, x] + part_in[chunk, :, r]
+
+    bins, cuts, pair_at, begin, mixed = plan(chunks, batches, per_batch)
+    count_items = batches * chunks
 
     def pick(t, table):
         value = 0
@@ -463,14 +467,13 @@
 
     def tick(t, carry):
         def at(lag, body):
-            when = [start + lag for start in starts]
-            found = pick(t, {k: 1 for k in when})
-            batch = pick(t, {k: item[0] for k, item in zip(when, items)})
-            step = pick(t, {k: item[1] for k, item in zip(when, items)})
-
-            @pl.when(found > 0)
+            start = begin + lag
+            k = jnp.minimum(jnp.maximum(t, start) - start, count_items - 1)
+            batch, chunk = nth_item(k, chunks, mixed)
+
+            @pl.when((t >= start) & (t < start + count_items))
             def _():
-                body(batch, step)
+                body(batch, chunk)
 
         at(LAG * bits, relay_stage)
         for stage in range(bits - 1, -1, -1):
@@ -500,26 +503,24 @@
         return carry
 
     pl.semaphore_wait(barrier, bits + 2)
-    lax.fori_loop(0, starts[-1] + LAG * bits + LAG + 1, tick, 0)
-
-    def finish_early(step, carry):
-        finish(step)
+    lax.fori_loop(0, begin + count_items + LAG * bits + LAG, tick, 0)
+
+    def finish_early(chunk, carry):
+        finish(chunk)
         return carry
 
-    lax.fori_loop(0, steps - 1, finish_early, 0)
+    lax.fori_loop(0, chunks - 1, finish_early, 0)
 
     all_first().wait_send()
     for stage in range(1, bits):
         all_half(stage).wait_send()
     all_raw(kz, 0).wait_send()
-    finish(steps - 1)
+    finish(chunks - 1)
 
     @pl.when(inner)
     def _():
         all_raw(outward, 1).wait_send()
         all_partial().wait_send()
-
-    pltpu.make_async_copy(out, out_hbm, out_sem.at[0]).wait()
 
 
 def per_device(kdata, spoke_angle, spoke_count, block_index, interp, sens_maps):
@@ -550,6 +551,7 @@
 
     chunks = steps * lanes
     block = (parts, 2, SUBLANE, LANE)
+    by_way = (2, parts // SUB, 2, SUBLANE, LANE)
     vmem = pltpu.VMEM
     scratch = [
         vmem((2, parts, spokes, samples), BF16),
@@ -565,23 +567,22 @@
         vmem((angles, spokes), F32),
         vmem((segs, angles * SUBLANE, seg), F32),
         vmem((batches, 2 * share * (hits + SUBLANE), seg), F32),
-        vmem((chunks, coils) + block, F32),
-        vmem((steps, groups, lanes) + block, F32),
-        vmem((steps, lanes) + block, F32),
-        vmem((steps, lanes) + block, F32),
+        vmem((chunks, coils) + by_way, F32),
+        vmem((chunks, groups) + by_way, F32),
+        vmem((chunks,) + block, F32),
+        vmem((chunks,) + block, F32),
     ]
-    scratch += [vmem((chunks, coils >> (s + 1)) + block, F32) for s in range(bits)]
+    scratch += [vmem((chunks, coils >> (s + 1)) + by_way, F32) for s in range(bits)]
     dma = pltpu.SemaphoreType.DMA
-    scratch += [vmem((2, parts, rows, side), F32)]
-    scratch += [dma((6,)), dma((batches,)), dma((CUTS,)), dma((1,))]
-    scratch += [dma((bits + 3,)), dma((batches, steps)), dma((bits - 1, batches, steps)), dma((2, batches, steps))]
+    scratch += [dma((6,)), dma((batches,)), dma((CUTS,))]
+    scratch += [dma((bits + 3,)), dma((batches, steps)), dma((bits - 1, batches, chunks)), dma((2, batches, chunks))]
     anywhere = pl.BlockSpec(memory_space=pltpu.HBM)
     dims = (bits, groups, parts, rows, side, angles, segs, seg, spokes)
     return pl.pallas_call(
         functools.partial(kernel, dims),
-        out_shape=jax.ShapeDtypeStruct((2, parts, rows, side), F32),
+        out_shape=pltpu.VMEM((2, parts, rows, side), F32),
         in_specs=[anywhere] * 8,
-        out_specs=anywhere,
+        out_specs=pl.BlockSpec(memory_space=pltpu.VMEM),
         scratch_shapes=scratch,
         compiler_params=pltpu.CompilerParams(
             collective_id=0, has_side_effects=True, vmem_limit_bytes=60 * 1024 * 1024

time: 80.1 us -> 74.6 us (0.931)
  Pallas kernels: 77.6 us -> 73.4 us
  local copies, waits for them, and re-layouts: 2.31 us -> 0.97 us
    pallas_call x1, Pallas kernels: 77.6 us -> 73.4 us  [per_device(): pl.pallas_call(functools.partial(kernel, dims), out_shape=pltpu.VMEM((2,...]
    unnamed x1, local copies, waits for them, and re-layouts: 2.31 us -> 0.97 us
where the time goes in v2:
time: 74.6 us; the launch traced here: 74.4 us
  Pallas kernels  73.4 us (98%)
  local copies, waits for them, and re-layouts  0.97 us (1%)
    pallas_call x1, Pallas kernels, per_device(): pl.pallas_call(functools.partial(kernel, dims), out_shape=pltpu.VMEM((2,...  73.4 us

profile of v2, /device:TPU:0, one launch (start us, length us, event | category | flops | bytes accessed | tf_op | source)
XLA Modules:
  0.0 74.4 jit_solution(12591418818109226569)
XLA Ops:
  0.0 73.4 %reconstruct.1 = f32[2,16,32,256]{3,2,1,0:T(8,128)S(1)} custom-call(bf16[2,16,256,512]{3,2,1,0:T(8,128)(2,1)} %bitcast.4, s32[1,256]{1,0:T(1,128)} %bitcast.7, s32[16]{0:T(128)} %refs_2_.1, s32[4,64]{1,0:T(4,128)} %bitcast.6, bf16[64,4,128,128]{3,2,1,0:T(8,128)(2,1)} %refs_4_.1, bf16[2,256,256]{2,1,0:T(8,128)(2,1)} %bitcast.5, ...), custom_call_target="tpu_custom_call" | custom-call | tf_op jit(solution)/shard_map/reconstruct/pallas_call | solution.py:581
  73.4 1.0 %copy.10 = f32[2,16,32,256]{3,2,1,0:T(8,128)} copy(f32[2,16,32,256]{3,2,1,0:T(8,128)S(1)} %reconstruct.1) | data formatting | bytes 2097152

commit v3 on v2

--- a/solution.py
+++ b/solution.py
@@ -16,6 +16,7 @@
 SUBLANE, LANE = 8, 128
 CUTS = 4
 LAG = 3
+HALF_SLOTS, INNER_SLOTS = 8, 16
 
 
 def cos_sin(product, length):
@@ -62,7 +63,7 @@
     weighted, raw, part_out, part_in = refs[22:26]
     inbox = refs[26 : 26 + bits]
     small_sem, data_sem, interp_sem = refs[26 + bits : 29 + bits]
-    sent, first_recv, half_recv, line_recv = refs[29 + bits :]
+    sent, first_recv, half_recv, outer_recv, inner_recv = refs[29 + bits :]
     blocks = 1 << bits
     orders = halving_orders(bits)
     lanes = side // LANE
@@ -105,8 +106,6 @@
     data_copy(0).start()
     for copy in smalls[2:]:
         copy.start()
-    for cut in range(2):
-        interp_copy(cut).start()
 
     barrier = pltpu.get_barrier_semaphore()
     for bit in range(bits):
@@ -119,13 +118,12 @@
 
     for copy in smalls[:2]:
         copy.wait()
+    interp_copy(0).start()
     match[...] = (angle[...] == lax.broadcasted_iota(I32, (angles, spokes), 0)).astype(F32)
     for copy in smalls[2:]:
         copy.wait()
-    for cut in range(2, CUTS):
+    for cut in range(1, CUTS):
         interp_copy(cut).start()
-    for batch in range(1, batches):
-        data_copy(batch).start()
     across = side // seg
     row = lax.broadcasted_iota(I32, (side, hits), 0) * across
     hit_at = jnp.concatenate([where[g : g + 1, :] for g in range(segs)], axis=1)
@@ -156,32 +154,35 @@
     def of(batch):
         return pl.ds(batch * per_batch, per_batch)
 
-    def first_copy(step, span, arrived):
+    def first_of_step(step, span):
         chunk = pl.ds(step * lanes, lanes)
         return pltpu.make_async_remote_copy(
             src_ref=weighted.at[chunk, pl.ds((1 - my_bit[0]) * half, half), :, span],
             dst_ref=inbox[0].at[chunk, :, :, span],
             send_sem=sent.at[0],
-            recv_sem=first_recv.at[arrived, step],
+            recv_sem=first_recv.at[step],
             device_id={"coil": partner[0]},
         )
 
-    def first_of_pair(pair, step):
-        return first_copy(step, pl.ds(pair, 1), pair // per_batch)
-
-    def first_of_batch(batch, step):
-        return first_copy(step, of(batch), batch)
+    def first_whole(batch, span):
+        return pltpu.make_async_remote_copy(
+            src_ref=weighted.at[:, pl.ds((1 - my_bit[0]) * half, half), :, span],
+            dst_ref=inbox[0].at[:, :, :, span],
+            send_sem=sent.at[0],
+            recv_sem=first_recv.at[steps + batch],
+            device_id={"coil": partner[0]},
+        )
 
     def all_first():
         return pltpu.make_async_remote_copy(
             src_ref=weighted.at[:, pl.ds(0, half)],
             dst_ref=inbox[0],
             send_sem=sent.at[0],
-            recv_sem=first_recv.at[0, 0],
+            recv_sem=first_recv.at[0],
             device_id={"coil": partner[0]},
         )
 
-    def half_copy(batch, chunk, way, stage):
+    def half_copy(batch, chunk, k, way, stage):
         order = orders[way]
         bit = order[stage]
         size = blocks >> (stage + 1)
@@ -190,16 +191,16 @@
             src_ref=weighted.at[chunk, pl.ds(start, size), way, of(batch)],
             dst_ref=inbox[stage].at[chunk, :, way, of(batch)],
             send_sem=sent.at[stage],
-            recv_sem=half_recv.at[stage - 1, batch, chunk],
+            recv_sem=half_recv.at[stage - 1, lax.rem(k, HALF_SLOTS)],
             device_id={"coil": partner[bit]},
         )
 
-    def both_halves(batch, chunk, stage):
+    def both_halves(batch, chunk, k, stage):
         return pltpu.make_async_remote_copy(
             src_ref=weighted.at[chunk, pl.ds(0, blocks >> (stage + 1)), :, of(batch)],
             dst_ref=inbox[stage].at[chunk, :, :, of(batch)],
             send_sem=sent.at[stage],
-            recv_sem=half_recv.at[stage - 1, batch, chunk],
+            recv_sem=half_recv.at[stage - 1, lax.rem(k, HALF_SLOTS)],
             device_id={"coil": partner[stage]},
         )
 
@@ -208,7 +209,7 @@
             src_ref=weighted.at[:, pl.ds(0, blocks >> (stage + 1))],
             dst_ref=inbox[stage],
             send_sem=sent.at[stage],
-            recv_sem=half_recv.at[stage - 1, 0, 0],
+            recv_sem=half_recv.at[stage - 1, 0],
             device_id={"coil": partner[stage]},
         )
 
@@ -222,31 +223,31 @@
             else:
                 raw[chunk, kz, way, of(batch)] = total
 
-    def raw_copy(batch, chunk, source, leaves, lands):
+    def raw_copy(batch, chunk, source, leaves, landed):
         return pltpu.make_async_remote_copy(
             src_ref=raw.at[chunk, source, :, of(batch)],
             dst_ref=raw.at[chunk, source, :, of(batch)],
             send_sem=sent.at[bits + leaves],
-            recv_sem=line_recv.at[lands, batch, chunk],
+            recv_sem=landed,
             device_id={"kz": inward},
         )
 
-    def from_outer(batch, chunk, source):
-        return raw_copy(batch, chunk, source, 0, 0)
-
-    def from_inner(batch, chunk, source):
-        return raw_copy(batch, chunk, source, 0, 1)
-
-    def forward(batch, chunk, source):
-        return raw_copy(batch, chunk, source, 1, 1)
-
-    def far_side(batch, chunk):
+    def from_outer(batch, chunk, k, source):
+        return raw_copy(batch, chunk, source, 0, outer_recv.at[k])
+
+    def from_inner(batch, chunk, k, source):
+        return raw_copy(batch, chunk, source, 0, inner_recv.at[lax.rem(k, INNER_SLOTS)])
+
+    def forward(batch, chunk, k, source):
+        return raw_copy(batch, chunk, source, 1, inner_recv.at[lax.rem(k, INNER_SLOTS)])
+
+    def far_side(batch, chunk, k):
         far = pl.ds(jnp.where(kz < 2, 2, 0), 2)
         return pltpu.make_async_remote_copy(
             src_ref=raw.at[chunk, far, :, of(batch)],
             dst_ref=raw.at[chunk, far, :, of(batch)],
             send_sem=sent.at[bits],
-            recv_sem=line_recv.at[1, batch, chunk],
+            recv_sem=inner_recv.at[lax.rem(k, INNER_SLOTS)],
             device_id={"kz": inward},
         )
 
@@ -255,7 +256,7 @@
             src_ref=raw.at[:, source],
             dst_ref=raw.at[:, source],
             send_sem=sent.at[bits + leaves],
-            recv_sem=line_recv.at[0, 0, 0],
+            recv_sem=outer_recv.at[0],
             device_id={"kz": inward},
         )
 
@@ -264,7 +265,7 @@
             src_ref=part_out.at[chunk],
             dst_ref=part_in.at[chunk],
             send_sem=sent.at[bits + 2],
-            recv_sem=line_recv.at[0, 0, chunk],
+            recv_sem=outer_recv.at[chunk],
             device_id={"kz": outward},
         )
 
@@ -273,7 +274,7 @@
             src_ref=part_out,
             dst_ref=part_in,
             send_sem=sent.at[bits + 2],
-            recv_sem=line_recv.at[0, 0, 0],
+            recv_sem=outer_recv.at[0],
             device_id={"kz": outward},
         )
 
@@ -395,33 +396,38 @@
 
         return load, store
 
-    def reduce_stage(stage, batch, chunk):
+    def reduce_stage(stage, batch, chunk, k):
         if stage == 0:
 
-            @pl.when(lax.rem(chunk, lanes) == 0)
+            @pl.when((batch == 0) & (lax.rem(chunk, lanes) == 0))
             def _():
-                first_of_batch(batch, lax.div(chunk, lanes)).wait_recv()
+                first_of_step(lax.div(chunk, lanes), of(0)).wait_recv()
+
+            @pl.when((batch > 0) & (chunk == 0))
+            def _():
+                first_whole(batch, of(batch)).wait_recv()
+
         else:
-            both_halves(batch, chunk, stage).wait_recv()
+            both_halves(batch, chunk, k, stage).wait_recv()
         for way in range(2):
             add_inbox(batch, chunk, way, stage)
             if stage < bits - 1:
-                half_copy(batch, chunk, way, stage + 1).start()
+                half_copy(batch, chunk, k, way, stage + 1).start()
         if stage == bits - 1:
 
             @pl.when(outer)
             def _():
-                from_outer(batch, chunk, kz).start()
+                from_outer(batch, chunk, k, kz).start()
 
             @pl.when(inner)
             def _():
-                from_inner(batch, chunk, kz).start()
-
-    def relay_stage(batch, chunk):
+                from_inner(batch, chunk, k, kz).start()
+
+    def relay_stage(batch, chunk, k):
         @pl.when(inner)
         def _():
-            from_outer(batch, chunk, outward).wait_recv()
-            forward(batch, chunk, outward).start()
+            from_outer(batch, chunk, k, outward).wait_recv()
+            forward(batch, chunk, k, outward).start()
 
         for end in (0, last):
 
@@ -429,10 +435,10 @@
             def _(end=end):
                 transform(batch, chunk, [end], kz, *in_out(chunk))
 
-    def combine_stage(batch, chunk):
+    def combine_stage(batch, chunk, k):
         @pl.when(inner)
         def _():
-            far_side(batch, chunk).wait_recv()
+            far_side(batch, chunk, k).wait_recv()
 
         for place, end in ((1, 0), (last - 1, last)):
 
@@ -473,7 +479,7 @@
 
             @pl.when((t >= start) & (t < start + count_items))
             def _():
-                body(batch, chunk)
+                body(batch, chunk, k)
 
         at(LAG * bits, relay_stage)
         for stage in range(bits - 1, -1, -1):
@@ -490,12 +496,27 @@
             return carry
 
         lax.fori_loop(low, high, one_cut, 0)
+
+        @pl.when(t == 0)
+        def _():
+            for later in range(1, batches):
+                data_copy(later).start()
+
         first, end = [pick(t, {k: v[i] for k, v in pair_at.items()}) for i in range(2)]
 
         def one_pair(pair, carry):
             compute(pair)
-            for step in range(steps):
-                first_of_pair(pair, step).start()
+            batch = pair // per_batch
+
+            @pl.when(batch == 0)
+            def _():
+                for step in range(steps):
+                    first_of_step(step, pl.ds(pair, 1)).start()
+
+            @pl.when(batch > 0)
+            def _():
+                first_whole(batch, pl.ds(pair, 1)).start()
+
             return carry
 
         lax.fori_loop(first, end, one_pair, 0)
@@ -575,7 +596,8 @@
     scratch += [vmem((chunks, coils >> (s + 1)) + by_way, F32) for s in range(bits)]
     dma = pltpu.SemaphoreType.DMA
     scratch += [dma((6,)), dma((batches,)), dma((CUTS,))]
-    scratch += [dma((bits + 3,)), dma((batches, steps)), dma((bits - 1, batches, chunks)), dma((2, batches, chunks))]
+    scratch += [dma((bits + 3,)), dma((steps + batches,)), dma((bits - 1, HALF_SLOTS))]
+    scratch += [dma((batches * chunks,)), dma((INNER_SLOTS,))]
     anywhere = pl.BlockSpec(memory_space=pltpu.HBM)
     dims = (bits, groups, parts, rows, side, angles, segs, seg, spokes)
     return pl.pallas_call(

time: 74.6 us -> 72.4 us (0.971)
  Pallas kernels: 73.4 us -> 71.3 us
    pallas_call x1, Pallas kernels: 73.4 us -> 71.3 us  [per_device(): pl.pallas_call(functools.partial(kernel, dims), out_shape=pltpu.VMEM((2,...]
where the time goes in v3:
time: 72.4 us; the launch traced here: 72.3 us
  Pallas kernels  71.3 us (98%)
  local copies, waits for them, and re-layouts  0.97 us (1%)
    pallas_call x1, Pallas kernels, per_device(): pl.pallas_call(functools.partial(kernel, dims), out_shape=pltpu.VMEM((2,...  71.3 us

profile of v3, /device:TPU:0, one launch (start us, length us, event | category | flops | bytes accessed | tf_op | source)
XLA Modules:
  0.0 72.3 jit_solution(3740148494793697500)
XLA Ops:
  0.0 71.3 %reconstruct.1 = f32[2,16,32,256]{3,2,1,0:T(8,128)S(1)} custom-call(bf16[2,16,256,512]{3,2,1,0:T(8,128)(2,1)} %bitcast.4, s32[1,256]{1,0:T(1,128)} %bitcast.7, s32[16]{0:T(128)} %refs_2_.1, s32[4,64]{1,0:T(4,128)} %bitcast.6, bf16[64,4,128,128]{3,2,1,0:T(8,128)(2,1)} %refs_4_.1, bf16[2,256,256]{2,1,0:T(8,128)(2,1)} %bitcast.5, ...), custom_call_target="tpu_custom_call" | custom-call | tf_op jit(solution)/shard_map/reconstruct/pallas_call | solution.py:603
  71.3 1.0 %copy.10 = f32[2,16,32,256]{3,2,1,0:T(8,128)} copy(f32[2,16,32,256]{3,2,1,0:T(8,128)S(1)} %reconstruct.1) | data formatting | bytes 2097152

commit v4 on v3

--- a/solution.py
+++ b/solution.py
@@ -16,7 +16,7 @@
 SUBLANE, LANE = 8, 128
 CUTS = 4
 LAG = 3
-HALF_SLOTS, INNER_SLOTS = 8, 16
+HALF_SLOTS, INNER_SLOTS = 6, 10
 
 
 def cos_sin(product, length):
@@ -47,9 +47,8 @@
 def nth_item(k, chunks, mixed):
     if not mixed:
         return lax.div(k, chunks), lax.rem(k, chunks)
-    a, b, c = [jnp.maximum(k, first) - first for first in (8, 20, 26)]
-    late_batch = jnp.where(k < 26, 1 + lax.div(b, 2), 1 + lax.rem(c, 3))
-    late_chunk = jnp.where(k < 26, 4 + lax.rem(b, 2), 6 + lax.div(c, 3))
+    a, b = [jnp.maximum(k, first) - first for first in (8, 20)]
+    late_batch, late_chunk = 1 + lax.rem(b, 3), 4 + lax.div(b, 3)
     batch = jnp.where(k < 8, 0, jnp.where(k < 20, 1 + lax.div(a, 4), late_batch))
     chunk = jnp.where(k < 8, k, jnp.where(k < 20, lax.rem(a, 4), late_chunk))
     return batch, chunk
@@ -104,6 +103,7 @@
     for copy in smalls[:2]:
         copy.start()
     data_copy(0).start()
+    interp_copy(0).start()
     for copy in smalls[2:]:
         copy.start()
 
@@ -118,12 +118,11 @@
 
     for copy in smalls[:2]:
         copy.wait()
-    interp_copy(0).start()
+    for cut in range(1, CUTS):
+        interp_copy(cut).start()
     match[...] = (angle[...] == lax.broadcasted_iota(I32, (angles, spokes), 0)).astype(F32)
     for copy in smalls[2:]:
         copy.wait()
-    for cut in range(1, CUTS):
-        interp_copy(cut).start()
     across = side // seg
     row = lax.broadcasted_iota(I32, (side, hits), 0) * across
     hit_at = jnp.concatenate([where[g : g + 1, :] for g in range(segs)], axis=1)
@@ -520,7 +519,7 @@
             return carry
 
         lax.fori_loop(first, end, one_pair, 0)
-        at(LAG * bits + LAG, combine_stage)
+        at(LAG * bits + 2, combine_stage)
         return carry
 
     pl.semaphore_wait(barrier, bits + 2)

time: 72.4 us -> 72.3 us (level)
  no operation moved by 1% of the time
where the time goes in v4:
time: 72.3 us; the launch traced here: 72.1 us
  Pallas kernels  71.2 us (98%)
  local copies, waits for them, and re-layouts  0.97 us (1%)
    pallas_call x1, Pallas kernels, per_device(): pl.pallas_call(functools.partial(kernel, dims), out_shape=pltpu.VMEM((2,...  71.2 us

profile of v4, /device:TPU:0, one launch (start us, length us, event | category | flops | bytes accessed | tf_op | source)
XLA Modules:
  0.0 72.1 jit_solution(1017572776817966803)
XLA Ops:
  0.0 71.2 %reconstruct.1 = f32[2,16,32,256]{3,2,1,0:T(8,128)S(1)} custom-call(bf16[2,16,256,512]{3,2,1,0:T(8,128)(2,1)} %bitcast.4, s32[1,256]{1,0:T(1,128)} %bitcast.7, s32[16]{0:T(128)} %refs_2_.1, s32[4,64]{1,0:T(4,128)} %bitcast.6, bf16[64,4,128,128]{3,2,1,0:T(8,128)(2,1)} %refs_4_.1, bf16[2,256,256]{2,1,0:T(8,128)(2,1)} %bitcast.5, ...), custom_call_target="tpu_custom_call" | custom-call | tf_op jit(solution)/shard_map/reconstruct/pallas_call | solution.py:602
  71.2 1.0 %copy.10 = f32[2,16,32,256]{3,2,1,0:T(8,128)} copy(f32[2,16,32,256]{3,2,1,0:T(8,128)S(1)} %reconstruct.1) | data formatting | bytes 2097152
